TPU v7x, 32 devices: a whole 2x2x4 slice. The times are simulated.
32 devices in a mesh: pb: 4 (over z), ka: 8 (over y, x, core).
Axes of the slice: x: 2, y: 2, z: 4, core: 2. Of those that a mesh axis runs over, the one named last changes fastest.
Arguments:
- queries: float32 [1, 4096, 128], P(None, ('pb', 'ka')), may hold values from -6 to 6
- keys: float32 [1, 4096, 128], P(None, ('ka', 'pb')), may hold values from -6 to 6
- values: float32 [1, 4096, 128], P(None, ('ka', 'pb')), may hold values from -6 to 6
- tangent_q: float32 [1, 4096, 128], P(None, ('pb', 'ka')), may hold values from -6 to 6
- tangent_k: float32 [1, 4096, 128], P(None, ('ka', 'pb')), may hold values from -6 to 6
- tangent_v: float32 [1, 4096, 128], P(None, ('ka', 'pb')), may hold values from -6 to 6
Outputs:
- attended: float32 [1, 4096, 128], P(None, ('pb', 'ka'))
- attended_tangent: float32 [1, 4096, 128], P(None, ('pb', 'ka'))
All inputs are finite; a program needn't handle non-finite values.
Results may differ from a plain program's by a relative error of at most 0.0003.
Values sent between devices are 32-bit elements; how exact they have to be, the bound alone decides.
No kernel may reach another device: no remote copies, remote signals or barrier semaphores. Data moves between devices by JAX's collectives and lax.ppermute only.
A program may use at most 128 MiB of HBM per device.

v0:
```python
import jax
import jax.numpy as jnp
from jax import lax
from jax.sharding import PartitionSpec as P


def combined_all(value, axis, join):
    pieces = jax.tree.map(lambda part: lax.all_gather(part, axis), value)
    head = jax.tree.map(lambda part: part[0], pieces)
    tail = jax.tree.map(lambda part: part[1:], pieces)
    so_far, _ = lax.scan(lambda so_far, share: (join(so_far, share), None), head, tail)
    return so_far


def join_partials(first, second):
    peak = jnp.maximum(first[0], second[0])
    left = jnp.exp(first[0] - peak)
    right = jnp.exp(second[0] - peak)
    total = first[1] * left + second[1] * right
    numer = first[2] * left[..., None] + second[2] * right[..., None]
    tnumer = first[3] * left[..., None] + second[3] * right[..., None]
    drift = first[4] * left + second[4] * right
    return (peak, total, numer, tnumer, drift)


def body(queries, keys, values, tangent_q, tangent_k, tangent_v):
    highest = lax.Precision.HIGHEST
    head_count, _, width = queries.shape
    factor = width ** (-0.5)
    all_q, all_dq = (
        lax.all_gather(queries, "ka", axis=1, tiled=True),
        lax.all_gather(tangent_q, "ka", axis=1, tiled=True),
    )
    span = all_q.shape[1]
    block = min(512, span)
    blocks = span // block
    split_q = all_q.reshape(head_count, blocks, block, width)
    split_dq = all_dq.reshape(head_count, blocks, block, width)
    start_state = (
        jnp.full((head_count, span), -1e30, jnp.float32),
        jnp.zeros((head_count, span), jnp.float32),
        jnp.zeros((head_count, span, width), jnp.float32),
        jnp.zeros((head_count, span, width), jnp.float32),
        jnp.zeros((head_count, span), jnp.float32),
    )
    piece_k = lax.all_gather(keys, "pb", axis=1, tiled=True)
    piece_dk = lax.all_gather(tangent_k, "pb", axis=1, tiled=True)
    piece_v = lax.all_gather(values, "pb", axis=1, tiled=True)
    piece_dv = lax.all_gather(tangent_v, "pb", axis=1, tiled=True)
    shaped = (
        start_state[0].reshape(head_count, blocks, block),
        start_state[1].reshape(head_count, blocks, block),
        start_state[2].reshape(head_count, blocks, block, width),
        start_state[3].reshape(head_count, blocks, block, width),
        start_state[4].reshape(head_count, blocks, block),
    )

    def one_head(items):
        (
            head_q,
            head_dq,
            head_k,
            head_dk,
            head_v,
            head_dv,
            peak_h,
            total_h,
            numer_h,
            tnumer_h,
            drift_h,
        ) = items

        def one_block(parts):
            query_blk, dquery_blk, old_peak, old_total, old_numer, old_tnumer, old_drift = parts
            scores = jnp.dot(query_blk, head_k.T, precision=highest) * factor
            tangent = (
                jnp.dot(dquery_blk, head_k.T, precision=highest)
                + jnp.dot(query_blk, head_dk.T, precision=highest)
            ) * factor
            new_peak = jnp.maximum(old_peak, jnp.max(scores, axis=1))
            rescale = jnp.exp(old_peak - new_peak)
            weights = jnp.exp(scores - new_peak[:, None])
            product = weights * tangent
            new_total = old_total * rescale + jnp.sum(weights, axis=1)
            new_numer = old_numer * rescale[:, None] + jnp.dot(weights, head_v, precision=highest)
            new_tnumer = (
                old_tnumer * rescale[:, None]
                + jnp.dot(weights, head_dv, precision=highest)
                + jnp.dot(product, head_v, precision=highest)
            )
            new_drift = old_drift * rescale + jnp.sum(product, axis=1)
            return (new_peak, new_total, new_numer, new_tnumer, new_drift)

        return lax.map(one_block, (head_q, head_dq, peak_h, total_h, numer_h, tnumer_h, drift_h))

    result = lax.map(one_head, (split_q, split_dq, piece_k, piece_dk, piece_v, piece_dv) + shaped)
    peak = result[0].reshape(head_count, span)
    total = result[1].reshape(head_count, span)
    numer = result[2].reshape(head_count, span, width)
    tnumer = result[3].reshape(head_count, span, width)
    drift = result[4].reshape(head_count, span)
    merged = combined_all((peak, total, numer, tnumer, drift), "ka", join_partials)
    owned = span // lax.axis_size("ka")
    offset = lax.axis_index("ka") * owned
    total = lax.dynamic_slice_in_dim(merged[1], offset, owned, 1)
    numer = lax.dynamic_slice_in_dim(merged[2], offset, owned, 1)
    tnumer = lax.dynamic_slice_in_dim(merged[3], offset, owned, 1)
    drift = lax.dynamic_slice_in_dim(merged[4], offset, owned, 1)
    attended = numer / total[..., None]
    attended_tangent = tnumer / total[..., None] - attended * (drift / total)[..., None]
    return (attended, attended_tangent)


def solution(mesh):
    return jax.shard_map(
        body,
        mesh=mesh,
        in_specs=(
            P(None, ("pb", "ka"), None),
            P(None, ("ka", "pb"), None),
            P(None, ("ka", "pb"), None),
            P(None, ("pb", "ka"), None),
            P(None, ("ka", "pb"), None),
            P(None, ("ka", "pb"), None),
        ),
        out_specs=(P(None, ("pb", "ka"), None), P(None, ("pb", "ka"), None)),
        check_vma=False,
    )
```

profile of v0, /device:TPU:0, one launch (start us, length us, event | category | flops | bytes accessed | tf_op | source)
XLA Modules:
  0.0 214.0 jit_solution(3527905628978141757)
XLA Ops:
  7.2 0.0 all-gather.5.cloned.1.call-start
  7.3 15.9 %all_gather.34 = f32[1,512,128]{2,1,0:T(8,128)S(1)} all-gather(f32[1,128,128]{2,1,0:T(8,128)} %param.11), channel_id=1, replica_groups=mesh['pb'=4,'ka'=8] {'pb'}, dimensions={1}, use_global_device_ids=true | all-gather | bytes 327680 | tf_op jit(solution)/shard_map/all_gather | solution.py:46
  23.1 14.9 %all_gather.35 = f32[1,512,128]{2,1,0:T(8,128)S(1)} all-gather(f32[1,128,128]{2,1,0:T(8,128)} %param.12), channel_id=1, replica_groups=mesh['pb'=4,'ka'=8] {'pb'}, dimensions={1}, use_global_device_ids=true | all-gather | bytes 327680 | tf_op jit(solution)/shard_map/all_gather | solution.py:48
  38.0 14.0 %all_gather.38 = f32[1,512,128]{2,1,0:T(8,128)S(1)} all-gather(f32[1,128,128]{2,1,0:T(8,128)} %param.14), channel_id=1, replica_groups=mesh['pb'=4,'ka'=8] {'pb'}, dimensions={1}, use_global_device_ids=true | all-gather | bytes 327680 | tf_op jit(solution)/shard_map/all_gather | solution.py:47
  52.1 16.6 %all_gather.36 = f32[1,512,128]{2,1,0:T(8,128)} all-gather(f32[1,128,128]{2,1,0:T(8,128)} %param.15), channel_id=1, replica_groups=mesh['pb'=4,'ka'=8] {'pb'}, dimensions={1}, use_global_device_ids=true | all-gather | bytes 327680 | tf_op jit(solution)/shard_map/all_gather | solution.py:49
  68.6 10.1 %all_gather.33 = f32[1,1024,128]{2,1,0:T(8,128)S(1)} all-gather(f32[1,128,128]{2,1,0:T(8,128)} %param.10), channel_id=1, replica_groups=mesh['pb'=4,'ka'=8] {'ka'}, dimensions={1}, use_global_device_ids=true | all-gather | bytes 589824 | tf_op jit(solution)/shard_map/all_gather | solution.py:31
  78.8 10.8 %all_gather.37 = f32[1,1024,128]{2,1,0:T(8,128)} all-gather(f32[1,128,128]{2,1,0:T(8,128)} %param.13), channel_id=1, replica_groups=mesh['pb'=4,'ka'=8] {'ka'}, dimensions={1}, use_global_device_ids=true | all-gather | bytes 589824 | tf_op jit(solution)/shard_map/all_gather | solution.py:32
  89.5 24.6 %while.53 = (s32[]{:T(128)}, f32[2,512]{1,0:T(2,128)S(1)}, f32[2,512]{1,0:T(2,128)S(1)}, f32[2,512,128]{2,1,0:T(8,128)}, f32[2,512,128]{2,1,0:T(8,128)}, /*index...) while((s32[]{:T(128)}, f32[2,512]{1,0:T(2,128)S(1)}, ...), condition=%wide.region_4.5_spmd, body=%wide.region_0.4_spmd.sunk | while | flops 2419001344 | bytes 12892333 | solution.py:94
  89.5 1.9 fusion.66
  91.5 1.0 fusion.65
  92.5 0.2 fusion.68
  92.7 1.2 fusion.67
  94.0 2.8 %convolution_add_fusion.5 = f32[512,128]{1,0:T(8,128)S(1)} fusion(f32[512,128]{1,0:T(8,128)} %get-tuple-element.549, f32[512,512]{0,1:T(8,128)S(1)} %get-tuple-element.489, f32[512]{0:T(512)S(1)} %get-tuple-element.488, f32[512]{0:T(512)S(1)} %get-tuple-element.492), kind=kOutput, calls=%fused_computation.7.clone.1 | convolution fusion | flops 402980864 | bytes 1576960 | tf_op jit(solution)/shard_map/while/body/eval_jaxpr/while/body/eval_jaxpr/dot_general | solution.py:88
  96.8 2.5 %fusion.71 = f32[2,512,128]{2,1,0:T(8,128)} fusion(f32[2,512,128]{2,1,0:T(8,128)} %get-tuple-element.530, s32[]{:T(128)S(6)} %copy.19, f32[512,128]{1,0:T(8,128)S(1)} %convolution_add_fusion.5, f32[512,512]{0,1:T(8,128)S(1)} %get-tuple-element.493, f32[512,128]{1,0:T(8,128)S(1)} %get-tuple-element.548), kind=kOutput, calls=%fused_computation.6.clone.1 | convolution fusion | flops 402718720 | bytes 1835012 | tf_op jit(solution)/shard_map/while/body/eval_jaxpr/while/body/eval_jaxpr/dot_general | solution.py:89
  99.3 2.5 %fusion.70 = f32[2,512,128]{2,1,0:T(8,128)} fusion(f32[2,512,128]{2,1,0:T(8,128)} %get-tuple-element.529, s32[]{:T(128)S(6)} %copy.19, f32[512,128]{1,0:T(8,128)S(1)} %get-tuple-element.548, f32[512,512]{0,1:T(8,128)S(1)} %get-tuple-element.489, f32[512]{0:T(512)S(1)} %get-tuple-element.488, f32[512]{0:T(512)S(1)} %get-tuple-element.492), kind=kOutput, calls=%fused_computation.10.clone.1 | convolution fusion | flops 402980864 | bytes 1576964 | tf_op jit(solution)/shard_map/while/body/eval_jaxpr/while/body/eval_jaxpr/dot_general | solution.py:85
  101.9 1.9 fusion.66
  103.8 1.0 fusion.65
  104.9 0.2 fusion.68
  105.1 1.2 fusion.67
  106.4 2.8 %convolution_add_fusion.5 = f32[512,128]{1,0:T(8,128)S(1)} fusion(f32[512,128]{1,0:T(8,128)} %get-tuple-element.549, f32[512,512]{0,1:T(8,128)S(1)} %get-tuple-element.489, f32[512]{0:T(512)S(1)} %get-tuple-element.488, f32[512]{0:T(512)S(1)} %get-tuple-element.492), kind=kOutput, calls=%fused_computation.7.clone.1 | convolution fusion | flops 402980864 | bytes 1576960 | tf_op jit(solution)/shard_map/while/body/eval_jaxpr/while/body/eval_jaxpr/dot_general | solution.py:88
  109.1 2.5 %fusion.71 = f32[2,512,128]{2,1,0:T(8,128)} fusion(f32[2,512,128]{2,1,0:T(8,128)} %get-tuple-element.530, s32[]{:T(128)S(6)} %copy.19, f32[512,128]{1,0:T(8,128)S(1)} %convolution_add_fusion.5, f32[512,512]{0,1:T(8,128)S(1)} %get-tuple-element.493, f32[512,128]{1,0:T(8,128)S(1)} %get-tuple-element.548), kind=kOutput, calls=%fused_computation.6.clone.1 | convolution fusion | flops 402718720 | bytes 1835012 | tf_op jit(solution)/shard_map/while/body/eval_jaxpr/while/body/eval_jaxpr/dot_general | solution.py:89
  111.7 2.5 %fusion.70 = f32[2,512,128]{2,1,0:T(8,128)} fusion(f32[2,512,128]{2,1,0:T(8,128)} %get-tuple-element.529, s32[]{:T(128)S(6)} %copy.19, f32[512,128]{1,0:T(8,128)S(1)} %get-tuple-element.548, f32[512,512]{0,1:T(8,128)S(1)} %get-tuple-element.489, f32[512]{0:T(512)S(1)} %get-tuple-element.488, f32[512]{0:T(512)S(1)} %get-tuple-element.492), kind=kOutput, calls=%fused_computation.10.clone.1 | convolution fusion | flops 402980864 | bytes 1576964 | tf_op jit(solution)/shard_map/while/body/eval_jaxpr/while/body/eval_jaxpr/dot_general | solution.py:85
  114.2 0.0 all-gather.5.cloned.1.call-update
  114.2 0.0 all-gather.3.cloned.1.call-start
  114.3 0.7 all-gather.3.cloned.1.call-update
  115.0 8.8 %all_gather.40 = f32[8,1,1024]{2,1,0:T(1,128)S(1)} all-gather(f32[1,1,1024]{2,1,0:T(1,128)S(1)} %all_gather_reshape.16), channel_id=1, replica_groups=mesh['pb'=4,'ka'=8] {'ka'}, dimensions={0}, use_global_device_ids=true | all-gather | bytes 36864 | tf_op jit(solution)/shard_map/all_gather | solution.py:8
  123.8 0.0 copy-start
  123.8 8.6 %all_gather.39 = f32[8,1,1024]{2,1,0:T(1,128)S(1)} all-gather(f32[1,1,1024]{2,1,0:T(1,128)S(1)} %all_gather_reshape.15), channel_id=1, replica_groups=mesh['pb'=4,'ka'=8] {'ka'}, dimensions={0}, use_global_device_ids=true | all-gather | bytes 36864 | tf_op jit(solution)/shard_map/all_gather | solution.py:8
  132.4 0.0 copy-start.1
  132.4 9.0 %all_gather.43 = f32[8,1,1024]{2,1,0:T(1,128)S(1)} all-gather(f32[1,1,1024]{2,1,0:T(1,128)S(1)} %all_gather_reshape.19), channel_id=1, replica_groups=mesh['pb'=4,'ka'=8] {'ka'}, dimensions={0}, use_global_device_ids=true | all-gather | bytes 36864 | tf_op jit(solution)/shard_map/all_gather | solution.py:8
  141.4 0.0 copy-start.2
  141.4 8.8 %all-gather.5.cloned.1.call-done = f32[8,1,1024,128]{3,2,1,0:T(8,128)} async-done(((f32[1,1,1024,128]{3,2,1,0:T(8,128)}), f32[8,1,1024,128]{3,2,1,0:T(8,128)}) %all-gather.5.cloned.1.call-update) | async-done | bytes 4194320 | tf_op jit(solution)/shard_map/all_gather | solution.py:8
  150.2 4.1 %slice.48 = f32[7,1,1024,128]{3,2,1,0:T(8,128)} slice(f32[8,1,1024,128]{3,2,1,0:T(8,128)} %all-gather.5.cloned.1.call-done), slice={[1:8], [0:1], [0:1024], [0:128]} | slice | bytes 7340032 | tf_op jit(solution)/shard_map/slice | solution.py:10
  154.3 1.1 slice_bitcast_fusion
  155.3 0.0 copy-done
  155.4 0.0 copy-done.1
  155.4 0.0 copy-done.2
  155.4 33.3 %all-gather.3.cloned.1.call-done = f32[8,1,1024,128]{3,2,1,0:T(8,128)} async-done(((f32[1,1,1024,128]{3,2,1,0:T(8,128)}), f32[8,1,1024,128]{3,2,1,0:T(8,128)}) %all-gather.3.cloned.1.call-update) | async-done | bytes 4194320 | tf_op jit(solution)/shard_map/all_gather | solution.py:8
  188.7 0.0 slice-start
  188.7 0.0 slice-start.1
  188.7 0.0 slice-start.2
  188.7 1.1 slice_bitcast_fusion.1
  189.8 4.1 %slice.47 = f32[7,1,1024,128]{3,2,1,0:T(8,128)} slice(f32[8,1,1024,128]{3,2,1,0:T(8,128)} %all-gather.3.cloned.1.call-done), slice={[1:8], [0:1], [0:1024], [0:128]} | slice | bytes 7340032 | tf_op jit(solution)/shard_map/slice | solution.py:10
  193.8 0.0 slice-done
  193.8 0.0 slice-done.1
  193.8 0.0 slice-done.2
  193.8 12.5 %while.54 = (s32[]{:T(128)}, f32[1,1024]{1,0:T(1,128)S(1)}, f32[1,1024]{1,0:T(1,128)S(1)}, f32[1,1024,128]{2,1,0:T(8,128)S(1)}, f32[1,1024,128]{2,1,0:T(8,128)S(...) while((s32[]{:T(128)}, f32[1,1024]{1,0:T(1,128)S(1)}, ...), condition=%wide.region_6.7_spmd, body=%wide.region_5.6_spmd.sunk | while | flops 795650 | bytes 3207305 | solution.py:11
  193.9 1.7 fusion.74
  195.7 1.7 fusion.74
  197.5 1.7 fusion.74
  199.3 1.7 fusion.74
  201.1 1.7 fusion.74
  202.9 1.7 fusion.74
  204.7 1.7 fusion.74
  206.4 0.7 multiply_subtract_fusion
  (36 shorter events, 0.8 us)
Async XLA Ops:
  7.2 143.0 %all-gather.5.cloned.1.call-start = ((), (), s32[]{:S(2)}) async-start(), calls=%async_computation.1 | async-start | bytes 4718592 | tf_op jit(solution)/shard_map/all_gather | solution.py:8
  114.2 74.5 %all-gather.3.cloned.1.call-start = ((), (), s32[]{:S(2)}) async-start(), calls=%async_computation | async-start | bytes 4718592 | tf_op jit(solution)/shard_map/all_gather | solution.py:8
  123.8 31.5 %copy-start = (f32[8,1,1024]{2,1,0:T(1,128)}, f32[8,1,1024]{2,1,0:T(1,128)S(1)}, u32[]{:S(2)}) copy-start(f32[8,1,1024]{2,1,0:T(1,128)S(1)} %all_gather.40) | copy-start | bytes 98308
  132.4 22.9 %copy-start.1 = (f32[8,1,1024]{2,1,0:T(1,128)}, f32[8,1,1024]{2,1,0:T(1,128)S(1)}, u32[]{:S(2)}) copy-start(f32[8,1,1024]{2,1,0:T(1,128)S(1)} %all_gather.39) | copy-start | bytes 98308
  141.4 13.9 %copy-start.2 = (f32[8,1,1024]{2,1,0:T(1,128)}, f32[8,1,1024]{2,1,0:T(1,128)S(1)}, u32[]{:S(2)}) copy-start(f32[8,1,1024]{2,1,0:T(1,128)S(1)} %all_gather.43) | copy-start | bytes 98308
  188.7 5.2 %slice-start = ((f32[8,1,1024]{2,1,0:T(1,128)}), f32[7,1,1024]{2,1,0:T(1,128)S(1)}, s32[]{:S(2)}) async-start(f32[8,1,1024]{2,1,0:T(1,128)} %copy-done), calls=%async_computation.2 | async-start | bytes 57344 | tf_op jit(solution)/shard_map/slice | solution.py:10
  188.7 5.2 %slice-start.1 = ((f32[8,1,1024]{2,1,0:T(1,128)}), f32[7,1,1024]{2,1,0:T(1,128)S(1)}, s32[]{:S(2)}) async-start(f32[8,1,1024]{2,1,0:T(1,128)} %copy-done.1), calls=%async_computation.3 | async-start | bytes 57344 | tf_op jit(solution)/shard_map/slice | solution.py:10
  188.7 5.2 %slice-start.2 = ((f32[8,1,1024]{2,1,0:T(1,128)}), f32[7,1,1024]{2,1,0:T(1,128)S(1)}, s32[]{:S(2)}) async-start(f32[8,1,1024]{2,1,0:T(1,128)} %copy-done.2), calls=%async_computation.4 | async-start | bytes 57344 | tf_op jit(solution)/shard_map/slice | solution.py:10
Sparse Core Ops, SparseCore 0:
  114.3 35.8 all-gather.4
  152.1 36.5 all-gather.2
where the time goes:
time: 215 us; the launch traced here: 214 us
  blocking collectives  109 us (51%)
  waiting for transfers between devices  42.8 us (20%)
  matrix products  23.9 us (11%)
  between operations  14.1 us (7%)
  other arithmetic  13.6 us (6%)
  local copies, waits for them, and re-layouts  10.6 us (5%)
    all_gather x2, waiting for transfers between devices, combined_all(): pieces = jax.tree.map(lambda part: lax.all_gather(part, axis), value)  42.1 us
    all_gather x3, blocking collectives, combined_all(): pieces = jax.tree.map(lambda part: lax.all_gather(part, axis), value)  26.4 us
    all_gather x1, blocking collectives, body(): piece_dv = lax.all_gather(tangent_v, 'pb', axis=1, tiled=True)  16.6 us
    all_gather x1, blocking collectives, body(): piece_k = lax.all_gather(keys, 'pb', axis=1, tiled=True)  15.9 us
    all_gather x1, blocking collectives, body(): piece_v = lax.all_gather(values, 'pb', axis=1, tiled=True)  14.9 us
    all_gather x1, blocking collectives, body(): piece_dk = lax.all_gather(tangent_k, 'pb', axis=1, tiled=True)  14 us
    add x7, other arithmetic, join_partials(): tnumer = first[3] * left[..., None] + second[3] * right[..., None]  11.9 us
    all_gather x1, blocking collectives, body(): lax.all_gather(tangent_q, 'ka', axis=1, tiled=True)  10.8 us
  transfers between devices with their start and end apart: 2, of which 2 were waited for; matrix products, arithmetic and copies ran while one was open for 2% of the time, Pallas kernels for 0%

commit v1 on v0

--- a/solution.py
+++ b/solution.py
@@ -46,7 +46,7 @@
     piece_k = lax.all_gather(keys, "pb", axis=1, tiled=True)
     piece_dk = lax.all_gather(tangent_k, "pb", axis=1, tiled=True)
     piece_v = lax.all_gather(values, "pb", axis=1, tiled=True)
-    piece_dv = lax.all_gather(tangent_v, "pb", axis=1, tiled=True)
+    piece_dv = jnp.concatenate(lax.all_gather(tangent_v, "pb"), axis=1)
     shaped = (
         start_state[0].reshape(head_count, blocks, block),
         start_state[1].reshape(head_count, blocks, block),

time: 215 us -> 215 us (level)
  no operation moved by 1% of the time
where the time goes in v1:
time: 215 us; the launch traced here: 214 us
  blocking collectives  109 us (51%)
  waiting for transfers between devices  42.8 us (20%)
  matrix products  23.9 us (11%)
  between operations  14.1 us (7%)
  other arithmetic  13.6 us (6%)
  local copies, waits for them, and re-layouts  10.6 us (5%)
    all_gather x2, waiting for transfers between devices, combined_all(): pieces = jax.tree.map(lambda part: lax.all_gather(part, axis), value)  42.1 us
    all_gather x3, blocking collectives, combined_all(): pieces = jax.tree.map(lambda part: lax.all_gather(part, axis), value)  26.4 us
    all_gather x1, blocking collectives, body(): piece_dv = jnp.concatenate(lax.all_gather(tangent_v, 'pb'), axis=1)  16.6 us
    all_gather x1, blocking collectives, body(): piece_k = lax.all_gather(keys, 'pb', axis=1, tiled=True)  15.9 us
    all_gather x1, blocking collectives, body(): piece_v = lax.all_gather(values, 'pb', axis=1, tiled=True)  14.9 us
    all_gather x1, blocking collectives, body(): piece_dk = lax.all_gather(tangent_k, 'pb', axis=1, tiled=True)  14 us
    add x7, other arithmetic, join_partials(): tnumer = first[3] * left[..., None] + second[3] * right[..., None]  11.9 us
    all_gather x1, blocking collectives, body(): lax.all_gather(tangent_q, 'ka', axis=1, tiled=True)  10.8 us
  transfers between devices with their start and end apart: 2, of which 2 were waited for; matrix products, arithmetic and copies ran while one was open for 2% of the time, Pallas kernels for 0%

profile of v1, /device:TPU:0, one launch (start us, length us, event | category | flops | bytes accessed | tf_op | source)
XLA Modules:
  0.0 214.0 jit_solution(3189630060393108370)
XLA Ops:
  7.2 0.0 all-gather.6.cloned.1.call-start
  7.3 15.9 %all_gather.37 = f32[1,512,128]{2,1,0:T(8,128)S(1)} all-gather(f32[1,128,128]{2,1,0:T(8,128)} %param.11), channel_id=1, replica_groups=mesh['pb'=4,'ka'=8] {'pb'}, dimensions={1}, use_global_device_ids=true | all-gather | bytes 327680 | tf_op jit(solution)/shard_map/all_gather | solution.py:46
  23.1 14.9 %all_gather.38 = f32[1,512,128]{2,1,0:T(8,128)S(1)} all-gather(f32[1,128,128]{2,1,0:T(8,128)} %param.12), channel_id=1, replica_groups=mesh['pb'=4,'ka'=8] {'pb'}, dimensions={1}, use_global_device_ids=true | all-gather | bytes 327680 | tf_op jit(solution)/shard_map/all_gather | solution.py:48
  38.0 14.0 %all_gather.42 = f32[1,512,128]{2,1,0:T(8,128)S(1)} all-gather(f32[1,128,128]{2,1,0:T(8,128)} %param.14), channel_id=1, replica_groups=mesh['pb'=4,'ka'=8] {'pb'}, dimensions={1}, use_global_device_ids=true | all-gather | bytes 327680 | tf_op jit(solution)/shard_map/all_gather | solution.py:47
  52.1 16.6 %all-gather = f32[4,128,128]{2,1,0:T(8,128)} all-gather(f32[1,128,128]{2,1,0:T(8,128)} %param.15), channel_id=2, replica_groups=mesh['pb'=4,'ka'=8] {'pb'}, dimensions={0}, use_global_device_ids=true | all-gather | bytes 327680 | tf_op jit(solution)/shard_map/all_gather | solution.py:49
  68.6 10.1 %all_gather.36 = f32[1,1024,128]{2,1,0:T(8,128)S(1)} all-gather(f32[1,128,128]{2,1,0:T(8,128)} %param.10), channel_id=1, replica_groups=mesh['pb'=4,'ka'=8] {'ka'}, dimensions={1}, use_global_device_ids=true | all-gather | bytes 589824 | tf_op jit(solution)/shard_map/all_gather | solution.py:31
  78.8 10.8 %all_gather.41 = f32[1,1024,128]{2,1,0:T(8,128)} all-gather(f32[1,128,128]{2,1,0:T(8,128)} %param.13), channel_id=1, replica_groups=mesh['pb'=4,'ka'=8] {'ka'}, dimensions={1}, use_global_device_ids=true | all-gather | bytes 589824 | tf_op jit(solution)/shard_map/all_gather | solution.py:32
  89.5 24.6 %while.53 = (s32[]{:T(128)}, f32[2,512]{1,0:T(2,128)S(1)}, f32[2,512]{1,0:T(2,128)S(1)}, f32[2,512,128]{2,1,0:T(8,128)}, f32[2,512,128]{2,1,0:T(8,128)}, /*index...) while((s32[]{:T(128)}, f32[2,512]{1,0:T(2,128)S(1)}, ...), condition=%wide.region_4.5_spmd, body=%wide.region_0.4_spmd.sunk | while | flops 2419001344 | bytes 12892333 | solution.py:94
  89.5 1.9 fusion.66
  91.5 1.0 fusion.65
  92.5 0.2 fusion.68
  92.7 1.2 fusion.67
  94.0 2.8 %convolution_add_fusion.5 = f32[512,128]{1,0:T(8,128)S(1)} fusion(f32[512,128]{1,0:T(8,128)} %get-tuple-element.549, f32[512,512]{0,1:T(8,128)S(1)} %get-tuple-element.489, f32[512]{0:T(512)S(1)} %get-tuple-element.488, f32[512]{0:T(512)S(1)} %get-tuple-element.492), kind=kOutput, calls=%fused_computation.7.clone.1 | convolution fusion | flops 402980864 | bytes 1576960 | tf_op jit(solution)/shard_map/while/body/eval_jaxpr/while/body/eval_jaxpr/dot_general | solution.py:88
  96.8 2.5 %fusion.71 = f32[2,512,128]{2,1,0:T(8,128)} fusion(f32[2,512,128]{2,1,0:T(8,128)} %get-tuple-element.530, s32[]{:T(128)S(6)} %copy.19, f32[512,128]{1,0:T(8,128)S(1)} %convolution_add_fusion.5, f32[512,512]{0,1:T(8,128)S(1)} %get-tuple-element.493, f32[512,128]{1,0:T(8,128)S(1)} %get-tuple-element.548), kind=kOutput, calls=%fused_computation.6.clone.1 | convolution fusion | flops 402718720 | bytes 1835012 | tf_op jit(solution)/shard_map/while/body/eval_jaxpr/while/body/eval_jaxpr/dot_general | solution.py:89
  99.3 2.5 %fusion.70 = f32[2,512,128]{2,1,0:T(8,128)} fusion(f32[2,512,128]{2,1,0:T(8,128)} %get-tuple-element.529, s32[]{:T(128)S(6)} %copy.19, f32[512,128]{1,0:T(8,128)S(1)} %get-tuple-element.548, f32[512,512]{0,1:T(8,128)S(1)} %get-tuple-element.489, f32[512]{0:T(512)S(1)} %get-tuple-element.488, f32[512]{0:T(512)S(1)} %get-tuple-element.492), kind=kOutput, calls=%fused_computation.10.clone.1 | convolution fusion | flops 402980864 | bytes 1576964 | tf_op jit(solution)/shard_map/while/body/eval_jaxpr/while/body/eval_jaxpr/dot_general | solution.py:85
  101.9 1.9 fusion.66
  103.8 1.0 fusion.65
  104.9 0.2 fusion.68
  105.1 1.2 fusion.67
  106.4 2.8 %convolution_add_fusion.5 = f32[512,128]{1,0:T(8,128)S(1)} fusion(f32[512,128]{1,0:T(8,128)} %get-tuple-element.549, f32[512,512]{0,1:T(8,128)S(1)} %get-tuple-element.489, f32[512]{0:T(512)S(1)} %get-tuple-element.488, f32[512]{0:T(512)S(1)} %get-tuple-element.492), kind=kOutput, calls=%fused_computation.7.clone.1 | convolution fusion | flops 402980864 | bytes 1576960 | tf_op jit(solution)/shard_map/while/body/eval_jaxpr/while/body/eval_jaxpr/dot_general | solution.py:88
  109.1 2.5 %fusion.71 = f32[2,512,128]{2,1,0:T(8,128)} fusion(f32[2,512,128]{2,1,0:T(8,128)} %get-tuple-element.530, s32[]{:T(128)S(6)} %copy.19, f32[512,128]{1,0:T(8,128)S(1)} %convolution_add_fusion.5, f32[512,512]{0,1:T(8,128)S(1)} %get-tuple-element.493, f32[512,128]{1,0:T(8,128)S(1)} %get-tuple-element.548), kind=kOutput, calls=%fused_computation.6.clone.1 | convolution fusion | flops 402718720 | bytes 1835012 | tf_op jit(solution)/shard_map/while/body/eval_jaxpr/while/body/eval_jaxpr/dot_general | solution.py:89
  111.7 2.5 %fusion.70 = f32[2,512,128]{2,1,0:T(8,128)} fusion(f32[2,512,128]{2,1,0:T(8,128)} %get-tuple-element.529, s32[]{:T(128)S(6)} %copy.19, f32[512,128]{1,0:T(8,128)S(1)} %get-tuple-element.548, f32[512,512]{0,1:T(8,128)S(1)} %get-tuple-element.489, f32[512]{0:T(512)S(1)} %get-tuple-element.488, f32[512]{0:T(512)S(1)} %get-tuple-element.492), kind=kOutput, calls=%fused_computation.10.clone.1 | convolution fusion | flops 402980864 | bytes 1576964 | tf_op jit(solution)/shard_map/while/body/eval_jaxpr/while/body/eval_jaxpr/dot_general | solution.py:85
  114.2 0.0 all-gather.6.cloned.1.call-update
  114.2 0.0 all-gather.4.cloned.1.call-start
  114.3 0.7 all-gather.4.cloned.1.call-update
  115.0 8.8 %all_gather.44 = f32[8,1,1024]{2,1,0:T(1,128)S(1)} all-gather(f32[1,1,1024]{2,1,0:T(1,128)S(1)} %all_gather_reshape.16), channel_id=1, replica_groups=mesh['pb'=4,'ka'=8] {'ka'}, dimensions={0}, use_global_device_ids=true | all-gather | bytes 36864 | tf_op jit(solution)/shard_map/all_gather | solution.py:8
  123.8 0.0 copy-start
  123.8 8.6 %all_gather.43 = f32[8,1,1024]{2,1,0:T(1,128)S(1)} all-gather(f32[1,1,1024]{2,1,0:T(1,128)S(1)} %all_gather_reshape.15), channel_id=1, replica_groups=mesh['pb'=4,'ka'=8] {'ka'}, dimensions={0}, use_global_device_ids=true | all-gather | bytes 36864 | tf_op jit(solution)/shard_map/all_gather | solution.py:8
  132.4 0.0 copy-start.1
  132.4 9.0 %all_gather.47 = f32[8,1,1024]{2,1,0:T(1,128)S(1)} all-gather(f32[1,1,1024]{2,1,0:T(1,128)S(1)} %all_gather_reshape.19), channel_id=1, replica_groups=mesh['pb'=4,'ka'=8] {'ka'}, dimensions={0}, use_global_device_ids=true | all-gather | bytes 36864 | tf_op jit(solution)/shard_map/all_gather | solution.py:8
  141.4 0.0 copy-start.2
  141.4 8.8 %all-gather.6.cloned.1.call-done = f32[8,1,1024,128]{3,2,1,0:T(8,128)} async-done(((f32[1,1,1024,128]{3,2,1,0:T(8,128)}), f32[8,1,1024,128]{3,2,1,0:T(8,128)}) %all-gather.6.cloned.1.call-update) | async-done | bytes 4194320 | tf_op jit(solution)/shard_map/all_gather | solution.py:8
  150.2 4.1 %slice.48 = f32[7,1,1024,128]{3,2,1,0:T(8,128)} slice(f32[8,1,1024,128]{3,2,1,0:T(8,128)} %all-gather.6.cloned.1.call-done), slice={[1:8], [0:1], [0:1024], [0:128]} | slice | bytes 7340032 | tf_op jit(solution)/shard_map/slice | solution.py:10
  154.3 1.1 slice_bitcast_fusion
  155.3 0.0 copy-done
  155.4 0.0 copy-done.1
  155.4 0.0 copy-done.2
  155.4 33.3 %all-gather.4.cloned.1.call-done = f32[8,1,1024,128]{3,2,1,0:T(8,128)} async-done(((f32[1,1,1024,128]{3,2,1,0:T(8,128)}), f32[8,1,1024,128]{3,2,1,0:T(8,128)}) %all-gather.4.cloned.1.call-update) | async-done | bytes 4194320 | tf_op jit(solution)/shard_map/all_gather | solution.py:8
  188.7 0.0 slice-start
  188.7 0.0 slice-start.1
  188.7 0.0 slice-start.2
  188.7 1.1 slice_bitcast_fusion.1
  189.8 4.1 %slice.47 = f32[7,1,1024,128]{3,2,1,0:T(8,128)} slice(f32[8,1,1024,128]{3,2,1,0:T(8,128)} %all-gather.4.cloned.1.call-done), slice={[1:8], [0:1], [0:1024], [0:128]} | slice | bytes 7340032 | tf_op jit(solution)/shard_map/slice | solution.py:10
  193.8 0.0 slice-done
  193.8 0.0 slice-done.1
  193.8 0.0 slice-done.2
  193.8 12.5 %while.54 = (s32[]{:T(128)}, f32[1,1024]{1,0:T(1,128)S(1)}, f32[1,1024]{1,0:T(1,128)S(1)}, f32[1,1024,128]{2,1,0:T(8,128)S(1)}, f32[1,1024,128]{2,1,0:T(8,128)S(...) while((s32[]{:T(128)}, f32[1,1024]{1,0:T(1,128)S(1)}, ...), condition=%wide.region_6.7_spmd, body=%wide.region_5.6_spmd.sunk | while | flops 795650 | bytes 3207305 | solution.py:11
  193.9 1.7 fusion.74
  195.7 1.7 fusion.74
  197.5 1.7 fusion.74
  199.3 1.7 fusion.74
  201.1 1.7 fusion.74
  202.9 1.7 fusion.74
  204.7 1.7 fusion.74
  206.4 0.7 multiply_subtract_fusion
  (36 shorter events, 0.8 us)
Async XLA Ops:
  7.2 143.0 %all-gather.6.cloned.1.call-start = ((), (), s32[]{:S(2)}) async-start(), calls=%async_computation.1 | async-start | bytes 4718592 | tf_op jit(solution)/shard_map/all_gather | solution.py:8
  114.2 74.5 %all-gather.4.cloned.1.call-start = ((), (), s32[]{:S(2)}) async-start(), calls=%async_computation | async-start | bytes 4718592 | tf_op jit(solution)/shard_map/all_gather | solution.py:8
  123.8 31.5 %copy-start = (f32[8,1,1024]{2,1,0:T(1,128)}, f32[8,1,1024]{2,1,0:T(1,128)S(1)}, u32[]{:S(2)}) copy-start(f32[8,1,1024]{2,1,0:T(1,128)S(1)} %all_gather.44) | copy-start | bytes 98308
  132.4 22.9 %copy-start.1 = (f32[8,1,1024]{2,1,0:T(1,128)}, f32[8,1,1024]{2,1,0:T(1,128)S(1)}, u32[]{:S(2)}) copy-start(f32[8,1,1024]{2,1,0:T(1,128)S(1)} %all_gather.43) | copy-start | bytes 98308
  141.4 13.9 %copy-start.2 = (f32[8,1,1024]{2,1,0:T(1,128)}, f32[8,1,1024]{2,1,0:T(1,128)S(1)}, u32[]{:S(2)}) copy-start(f32[8,1,1024]{2,1,0:T(1,128)S(1)} %all_gather.47) | copy-start | bytes 98308
  188.7 5.2 %slice-start = ((f32[8,1,1024]{2,1,0:T(1,128)}), f32[7,1,1024]{2,1,0:T(1,128)S(1)}, s32[]{:S(2)}) async-start(f32[8,1,1024]{2,1,0:T(1,128)} %copy-done), calls=%async_computation.2 | async-start | bytes 57344 | tf_op jit(solution)/shard_map/slice | solution.py:10
  188.7 5.2 %slice-start.1 = ((f32[8,1,1024]{2,1,0:T(1,128)}), f32[7,1,1024]{2,1,0:T(1,128)S(1)}, s32[]{:S(2)}) async-start(f32[8,1,1024]{2,1,0:T(1,128)} %copy-done.1), calls=%async_computation.3 | async-start | bytes 57344 | tf_op jit(solution)/shard_map/slice | solution.py:10
  188.7 5.2 %slice-start.2 = ((f32[8,1,1024]{2,1,0:T(1,128)}), f32[7,1,1024]{2,1,0:T(1,128)S(1)}, s32[]{:S(2)}) async-start(f32[8,1,1024]{2,1,0:T(1,128)} %copy-done.2), calls=%async_computation.4 | async-start | bytes 57344 | tf_op jit(solution)/shard_map/slice | solution.py:10
Sparse Core Ops, SparseCore 0:
  114.3 35.8 all-gather.5
  152.1 36.5 all-gather.3
